TPU v7x, 32 devices: a whole 2x2x4 slice. The times are simulated.
32 devices in a mesh: grp: 4 (over x, core), dev: 8 (over z, y).
Axes of the slice: x: 2, y: 2, z: 4, core: 2. Of those that a mesh axis runs over, the one named last changes fastest.
Arguments:
- node_features: float32 [16384, 768], P(('grp', 'dev')), may hold values from -6 to 6
- tiles: bfloat16 [896, 128, 128], P(('grp', 'dev')), may hold values from -0.1875 to 0.1875
- tile_list: int32 [896, 2], replicated, may hold values from 0 to 127, as said below
- weight: float32 [768, 768], replicated, may hold values from -0.21875 to 0.21875
- texts: float32 [1024, 768], P(('grp', 'dev')), may hold values from -6 to 6
- selected: int32 [1024], P(('grp', 'dev')), may hold values from 0 to 16383, as said below
- pairing: int32 [1024], P(('grp', 'dev')), may hold values from 0 to 1023, each once
Outputs:
- contrast_loss: float32 [], replicated
- grad_nodes: float32 [16384, 768], P(('grp', 'dev'))
- grad_weight: float32 [768, 768], replicated
- grad_texts: float32 [1024, 768], P(('grp', 'dev'))
Inputs may be any that keep to these rules, and one draw needn't show every extreme that they name: `tile_list`: device number p = grp index * (devices along dev) + dev index holds node blocks p * 4 to (p + 1) * 4 - 1 and tiles p * 28 to (p + 1) * 28 - 1. A tile's row block lies on the device that holds the tile; its column block lies on that device, on another device of the same grp index, or on the device of the same dev index in another grp. At most 2 tiles of one device have column blocks on any one other device; in every draw each device has one other device of its grp index and one of its dev index at that most. `selected`: distinct ids; the ids listed on a device are nodes of that device.
All inputs are finite; a program needn't handle non-finite values.
Results may differ from a plain program's by a relative error of at most 0.0004.
The roundings to bfloat16 on the way count: a program that leaves them out, or rounds other values in their place, can miss the bound.
Values may be sent and summed in bfloat16 or wider, within the bound.
No kernel may reach another device: no remote copies, remote signals or barrier semaphores. Data moves between devices by JAX's collectives and lax.ppermute only.
A program may use at most 128 MiB of HBM per device.

v0:
```python
import jax
import jax.numpy as jnp
from jax import lax
from jax.sharding import PartitionSpec as P

CAP = 2
SCALE = 1.0 / 0.07
EPS = 1e-06
PRECISE = lax.Precision.HIGHEST
ROOT_HALF = 0.7071067811865476
INV_ROOT_TWO_PI = 0.3989422804014327


def gelu_value(value):
    return 0.5 * value * (1.0 + lax.erf(value * ROOT_HALF))


def gelu_slope(value):
    return (
        0.5 * (1.0 + lax.erf(value * ROOT_HALF))
        + value * jnp.exp(-0.5 * value * value) * INV_ROOT_TWO_PI
    )


def slot_plan(peer_lists, peer_ids, device, blocks_dev, capacity):
    col_owner = peer_lists[:, :, 1] // blocks_dev
    wanted = (col_owner == device) & (peer_ids[:, None] != device)
    slot_order = jnp.cumsum(wanted.astype(jnp.int32), axis=1) - 1
    local_block = peer_lists[:, :, 1] - device * blocks_dev
    slot_hits = wanted[:, :, None] & (
        slot_order[:, :, None] == jnp.arange(capacity, dtype=jnp.int32)[None, None, :]
    )
    block_index = jnp.sum(jnp.where(slot_hits, local_block[:, :, None], 0), axis=1)
    slot_valid = jnp.any(slot_hits, axis=1)
    return (block_index.reshape(-1), slot_valid.reshape(-1))


def slot_pick(slot_of_tile, keep, slots_all):
    return (slot_of_tile[None, :] == jnp.arange(slots_all, dtype=jnp.int32)[:, None]) & keep[
        None, :
    ]


def land_blocks(total, block_index, valid, incoming):
    return total.at[block_index].add(jnp.where(valid[:, None, None], incoming, 0.0))


def shards(node_features, tiles, tile_list, weight, texts, selected, pairing):
    groups = lax.axis_size("grp")
    members = lax.axis_size("dev")
    grp_index = lax.axis_index("grp")
    dev_index = lax.axis_index("dev")
    device = grp_index * members + dev_index
    block_rows = tiles.shape[1]
    feat_width = node_features.shape[1]
    blocks_dev = node_features.shape[0] // block_rows
    tile_dev = tiles.shape[0]
    sel_dev = selected.shape[0]
    capacity = CAP
    total_sel = sel_dev * groups * members
    rounded = node_features.astype(jnp.bfloat16).reshape(blocks_dev, block_rows, feat_width)
    my_list = lax.dynamic_slice_in_dim(tile_list, device * tile_dev, tile_dev, 0)
    row_block = my_list[:, 0] - device * blocks_dev
    col_owner = my_list[:, 1] // blocks_dev
    col_block = my_list[:, 1] - col_owner * blocks_dev
    owner_grp = col_owner // members
    owner_dev = col_owner % members
    is_local = col_owner == device
    is_near = (owner_grp == grp_index) & jnp.logical_not(is_local)
    is_far = (owner_dev == dev_index) & (owner_grp != grp_index)
    positions = jnp.arange(tile_dev, dtype=jnp.int32)
    earlier = (col_owner[:, None] == col_owner[None, :]) & (positions[None, :] < positions[:, None])
    slot_rank = jnp.sum(earlier.astype(jnp.int32), axis=1)
    near_slot = owner_dev * capacity + slot_rank
    far_slot = owner_grp * capacity + slot_rank
    group_lists = lax.dynamic_slice_in_dim(
        tile_list, grp_index * members * tile_dev, members * tile_dev, 0
    ).reshape(members, tile_dev, 2)
    near_peers = grp_index * members + jnp.arange(members, dtype=jnp.int32)
    near_index, near_valid = slot_plan(group_lists, near_peers, device, blocks_dev, capacity)
    far_lists = lax.dynamic_index_in_dim(
        tile_list.reshape(groups, members, tile_dev, 2), dev_index, 1, False
    )
    far_peers = jnp.arange(groups, dtype=jnp.int32) * members + dev_index
    far_index, far_valid = slot_plan(far_lists, far_peers, device, blocks_dev, capacity)
    zero_half = jnp.zeros((), jnp.bfloat16)
    sel_local = selected - device * blocks_dev * block_rows
    sel_block = sel_local // block_rows
    sel_offset = sel_local % block_rows
    picked = jnp.take(tiles, sel_offset, axis=1)
    tile_rows = jnp.where((row_block[:, None] == sel_block[None, :])[:, :, None], picked, zero_half)
    near_pick = slot_pick(near_slot, is_near, members * capacity)
    far_pick = slot_pick(far_slot, is_far, groups * capacity)
    near_rows = jnp.einsum(
        "st,tkc->skc", near_pick.astype(jnp.bfloat16), tile_rows, preferred_element_type=jnp.float32
    ).astype(jnp.bfloat16)
    far_rows = jnp.einsum(
        "st,tkc->skc", far_pick.astype(jnp.bfloat16), tile_rows, preferred_element_type=jnp.float32
    ).astype(jnp.bfloat16)
    local_tile_rows = jnp.where(is_local[:, None, None], tile_rows, zero_half)
    near_send = jnp.where(
        near_valid[:, None, None], jnp.take(rounded, near_index, axis=0), zero_half
    )
    near_blocks = lax.all_to_all(
        near_send.reshape(members, capacity, block_rows, feat_width),
        "dev",
        split_axis=0,
        concat_axis=0,
        tiled=True,
    )
    far_send = jnp.where(far_valid[:, None, None], jnp.take(rounded, far_index, axis=0), zero_half)
    far_blocks = lax.all_to_all(
        far_send.reshape(groups, capacity, block_rows, feat_width),
        "grp",
        split_axis=0,
        concat_axis=0,
        tiled=True,
    )
    source_table = jnp.concatenate(
        [
            rounded,
            near_blocks.reshape(-1, block_rows, feat_width),
            far_blocks.reshape(-1, block_rows, feat_width),
        ],
        axis=0,
    )
    source_index = jnp.where(
        is_local,
        col_block,
        jnp.where(is_near, blocks_dev + near_slot, blocks_dev + members * capacity + far_slot),
    )
    sources = jnp.take(source_table, source_index, axis=0)
    messages = jnp.einsum("tkc,tcd->kd", tile_rows, sources, preferred_element_type=jnp.float32)
    chosen = node_features[sel_local] + messages
    before = jnp.dot(chosen, weight, precision=PRECISE)
    hidden = gelu_value(before)
    node_norm = jnp.sqrt(jnp.sum(hidden * hidden, axis=1, keepdims=True) + EPS)
    unit_nodes = hidden / node_norm
    text_norm = jnp.sqrt(jnp.sum(texts * texts, axis=1, keepdims=True) + EPS)
    unit_texts = texts / text_norm
    node_rows, pair_rows = (
        lax.all_gather(unit_nodes, "dev", axis=0, tiled=True),
        lax.all_gather(pairing, "dev", axis=0, tiled=True),
    )
    text_cols = lax.all_gather(unit_texts, "grp", axis=0, tiled=True)
    scores = SCALE * lax.dot_general(
        node_rows, text_cols, (((1,), (1,)), ((), ())), precision=PRECISE
    )
    exp_scores = jnp.exp(scores)
    row_total = lax.psum(jnp.sum(exp_scores, axis=1), "dev")
    col_total = lax.psum(jnp.sum(exp_scores, axis=0), "grp")
    col_global = (
        (jnp.arange(groups, dtype=jnp.int32)[:, None] * members + dev_index) * sel_dev
        + jnp.arange(sel_dev, dtype=jnp.int32)[None, :]
    ).reshape(-1)
    target = pair_rows[:, None] == col_global[None, :]
    score_grads = 0.5 * (
        exp_scores / row_total[:, None] + exp_scores / col_total[None, :]
    ) - target.astype(jnp.float32)
    node_part = SCALE * jnp.dot(score_grads, text_cols, precision=PRECISE)
    node_dir = lax.psum_scatter(node_part, "dev", scatter_dimension=0, tiled=True)
    text_part = SCALE * lax.dot_general(
        score_grads, node_rows, (((0,), (0,)), ((), ())), precision=PRECISE
    )
    text_dir = lax.psum_scatter(text_part, "grp", scatter_dimension=0, tiled=True)
    own_rows = lax.dynamic_slice_in_dim(row_total, dev_index * sel_dev, sel_dev, 0)
    own_cols = lax.dynamic_slice_in_dim(col_total, grp_index * sel_dev, sel_dev, 0)
    positive = jnp.sum(jnp.where(target, scores, 0.0))
    lse_sum, pos_sum = lax.psum(
        (jnp.sum(jnp.log(own_rows)) + jnp.sum(jnp.log(own_cols)), positive), ("grp", "dev")
    )
    contrast_loss = lse_sum / (2.0 * total_sel) - pos_sum / total_sel
    node_back = (
        node_dir - unit_nodes * jnp.sum(unit_nodes * node_dir, axis=1, keepdims=True)
    ) / node_norm
    grad_texts = (
        text_dir - unit_texts * jnp.sum(unit_texts * text_dir, axis=1, keepdims=True)
    ) / text_norm
    pre_grad = node_back * gelu_slope(before)
    weight_term = lax.dot_general(chosen, pre_grad, (((0,), (0,)), ((), ())), precision=PRECISE)
    grad_weight = lax.psum(weight_term, ("grp", "dev"))
    row_grads = lax.dot_general(pre_grad, weight, (((1,), (1,)), ((), ())), precision=PRECISE)
    rounded_grads = row_grads.astype(jnp.bfloat16)
    empty_blocks = jnp.zeros((blocks_dev, block_rows, feat_width), jnp.float32)
    local_spread = jnp.einsum(
        "tkc,kd->tcd", local_tile_rows, rounded_grads, preferred_element_type=jnp.float32
    )
    grad_blocks = empty_blocks.at[col_block].add(local_spread)
    near_rows_in = lax.all_to_all(
        near_rows.reshape(members, capacity, sel_dev, block_rows),
        "dev",
        split_axis=0,
        concat_axis=0,
        tiled=True,
    )
    near_grads_in = lax.all_gather(rounded_grads, "dev", axis=0, tiled=True).reshape(
        members, sel_dev, feat_width
    )
    near_spread = jnp.einsum(
        "pqkc,pkd->pqcd", near_rows_in, near_grads_in, preferred_element_type=jnp.float32
    )
    grad_blocks = land_blocks(
        grad_blocks, near_index, near_valid, near_spread.reshape(-1, block_rows, feat_width)
    )
    far_rows_in = lax.all_to_all(
        far_rows.reshape(groups, capacity, sel_dev, block_rows),
        "grp",
        split_axis=0,
        concat_axis=0,
        tiled=True,
    )
    far_grads_in = lax.all_gather(rounded_grads, "grp", axis=0, tiled=True).reshape(
        groups, sel_dev, feat_width
    )
    far_spread = jnp.einsum(
        "pqkc,pkd->pqcd", far_rows_in, far_grads_in, preferred_element_type=jnp.float32
    )
    grad_blocks = land_blocks(
        grad_blocks, far_index, far_valid, far_spread.reshape(-1, block_rows, feat_width)
    )
    grad_nodes = grad_blocks.reshape(-1, feat_width).at[sel_local].add(row_grads)
    return (contrast_loss, grad_nodes, grad_weight, grad_texts)


def solution(mesh):
    return jax.shard_map(
        shards,
        mesh=mesh,
        in_specs=(
            P(("grp", "dev"), None),
            P(("grp", "dev"), None, None),
            P(),
            P(),
            P(("grp", "dev"), None),
            P(("grp", "dev")),
            P(("grp", "dev")),
        ),
        out_specs=(P(), P(("grp", "dev"), None), P(), P(("grp", "dev"), None)),
        check_vma=False,
    )
```

profile of v0, /device:TPU:0, one launch (start us, length us, event | category | flops | bytes accessed | tf_op | source)
XLA Modules:
  0.0 443.1 jit_solution(16403538620831499144)
XLA Ops:
  15.3 4.4 all-to-all-start.1
  23.9 4.0 select_select_fusion
  27.9 12.5 %all-to-all-done.1 = bf16[4,2,128,768]{3,2,1,0:T(8,128)(2,1)} async-done(((bf16[4,2,128,768]{3,2,1,0:T(8,128)(2,1)}), bf16[4,2,128,768]{3,2,1,0:T(8,128)(2,1)}, u32[]{:S(2)}, u32[]{:S(2)}) %all-to-all-start.1) | async-done | bytes 1572896 | tf_op jit(solution)/shard_map/all_to_all | solution.py:112
  40.4 6.6 %all-to-all-start = ((bf16[8,2,128,768]{3,2,1,0:T(8,128)(2,1)}), bf16[8,2,128,768]{3,2,1,0:T(8,128)(2,1)}, u32[]{:S(2)}, u32[]{:S(2)}) async-start(bf16[8,2,128,768]{3,2,1,0:T(8,128)(2,1)} %select_select_fusion), calls=%async_computation | async-start | bytes 6291456 | tf_op jit(solution)/shard_map/all_to_all | solution.py:104
  53.7 64.1 %all-reduce = s32[256]{0:T(256)S(1)} all-reduce(s32[256]{0:T(256)S(1)} %dynamic-update-slice), channel_id=1, replica_groups=mesh['grp'=4,'dev'=8] {'dev'}, use_global_device_ids=true, to_apply=%add | all-reduce | flops 256 | bytes 2048
  119.0 6.6 %all_gather.16 = f32[128,768]{1,0:T(8,128)} all-gather(f32[32,768]{1,0:T(8,128)S(1)} %broadcast_divide_fusion), channel_id=1, replica_groups=mesh['grp'=4,'dev'=8] {'grp'}, dimensions={0}, use_global_device_ids=true | all-gather | bytes 491520 | tf_op jit(solution)/shard_map/all_gather | solution.py:145
  126.8 5.8 %pad_maximum_fusion = bf16[28,128,768]{2,1,0:T(8,128)(2,1)} fusion(bf16[8,128,768]{2,1,0:T(8,128)(2,1)} %bitcast.17, bf16[16,128,768]{2,1,0:T(8,128)(2,1)} %bitcast.11, bf16[4,128,768]{2,1,0:T(8,128)(2,1)S(1)} %bitcast.101), kind=kLoop, calls=%fused_computation.10 | loop fusion | flops 5505024 | bytes 11010048 | tf_op jit(solution)/shard_map/concatenate | solution.py:119
  132.6 6.0 %gather_fusion.4 = bf16[28,128,768]{2,1,0:T(8,128)(2,1)} fusion(bf16[28,128,768]{2,1,0:T(8,128)(2,1)} %pad_maximum_fusion, s32[1024]{0:T(1024)S(1)} %pad_clamp_fusion), kind=kCustom, calls=%fused_computation.4 | custom fusion | bytes 11010160 | tf_op jit(solution)/shard_map/jit(_take)/gather | solution.py:132
  138.6 3.6 fusion.7
  143.9 32.1 %all_gather.15 = f32[256,768]{1,0:T(8,128)S(1)} all-gather(f32[32,768]{1,0:T(8,128)S(1)} %broadcast_divide_fusion.1), channel_id=1, replica_groups=mesh['grp'=4,'dev'=8] {'dev'}, dimensions={0}, use_global_device_ids=true | all-gather | bytes 884736 | tf_op jit(solution)/shard_map/all_gather | solution.py:142
  178.0 19.6 %psum.35 = f32[256]{0:T(256)S(1)} all-reduce(f32[256]{0:T(256)S(1)} %get-tuple-element.6), channel_id=1, replica_groups=mesh['grp'=4,'dev'=8] {'dev'}, use_global_device_ids=true, to_apply=%region_10.11 | all-reduce | flops 256 | bytes 2048 | tf_op jit(solution)/shard_map/psum | solution.py:150
  197.6 5.6 %psum.36 = f32[128]{0:T(128)S(1)} all-reduce(f32[128]{0:T(128)S(1)} %get-tuple-element.5), channel_id=1, replica_groups=mesh['grp'=4,'dev'=8] {'grp'}, use_global_device_ids=true, to_apply=%region_13.14 | all-reduce | flops 128 | bytes 1024 | tf_op jit(solution)/shard_map/psum | solution.py:151
  216.5 40.7 %all-reduce.1 = (f32[]{:T(128)}, f32[]{:T(128)}) all-reduce(f32[]{:T(128)S(6)} %add.310, f32[]{:T(128)} %get-tuple-element.4), channel_id=1, replica_groups=mesh['grp'=4,'dev'=8] {'grp','dev'}, use_global_device_ids=true, to_apply=%region_15.16 | all-reduce | flops 2 | bytes 16 | tf_op jit(solution)/shard_map/psum | solution.py:169
  261.2 29.5 %reduce-scatter.3.cloned.1.call-done = f32[32,768]{1,0:T(8,128)} async-done(((f32[256,768]{1,0:T(8,128)}), f32[32,768]{1,0:T(8,128)}) %reduce-scatter.3.cloned.1.call-update) | async-done | bytes 98320 | tf_op jit(solution)/shard_map/reduce_scatter | solution.py:161
  291.9 4.4 fusion.57
  298.5 6.1 %fusion.12 = f32[28,128,768]{2,1,0:T(8,128)} fusion(bf16[28,32,128]{2,1,0:T(8,128)(2,1)S(1)} %bitcast_select_fusion.2, pred[28]{0:T(512)(128)(4,1)S(1)} %get-tuple-element.14, bf16[32,768]{1,0:T(8,128)(2,1)S(1)} %get-tuple-element.34), kind=kOutput, calls=%fused_computation.28 | convolution fusion | flops 176275456 | bytes 11288604 | tf_op jit(solution)/shard_map/tkc,kd->tcd/dot_general | solution.py:185
  305.9 25.5 %scatter_fusion = f32[4,128,768]{2,1,0:T(8,128)} fusion(f32[4,128,768]{2,1,0:T(8,128)} %broadcast_in_dim.214, s32[28]{0:T(128)S(1)} %get-tuple-element.15, f32[28,128,768]{2,1,0:T(8,128)} %fusion.12), kind=kCustom, calls=%fused_computation.5 | custom fusion | flops 2752512 | bytes 33030256 | tf_op jit(solution)/shard_map/scatter-add | solution.py:188
  331.4 31.2 %all_gather.18 = bf16[256,768]{1,0:T(8,128)(2,1)S(1)} all-gather(bf16[32,768]{1,0:T(8,128)(2,1)S(1)} %get-tuple-element.34), channel_id=1, replica_groups=mesh['grp'=4,'dev'=8] {'dev'}, dimensions={0}, use_global_device_ids=true | all-gather | bytes 442368 | tf_op jit(solution)/shard_map/all_gather | solution.py:196
  366.8 3.4 bitcast_select_fusion
  370.2 14.5 %scatter_fusion.1 = f32[4,128,768]{2,1,0:T(8,128)} fusion(f32[4,128,768]{2,1,0:T(8,128)} %scatter_fusion, s32[16]{0:T(128)S(1)} %fusion.47, f32[16,128,768]{2,1,0:T(8,128)} %bitcast_select_fusion), kind=kCustom, calls=%fused_computation.6 | custom fusion | flops 1572864 | bytes 18874432 | tf_op jit(solution)/shard_map/scatter-add | solution.py:45
  384.8 5.8 %all_gather.19 = bf16[128,768]{1,0:T(8,128)(2,1)S(1)} all-gather(bf16[32,768]{1,0:T(8,128)(2,1)S(1)} %get-tuple-element.34), channel_id=1, replica_groups=mesh['grp'=4,'dev'=8] {'grp'}, dimensions={0}, use_global_device_ids=true | all-gather | bytes 245760 | tf_op jit(solution)/shard_map/all_gather | solution.py:212
  393.2 7.4 %scatter_fusion.2 = f32[4,128,768]{2,1,0:T(8,128)} fusion(f32[4,128,768]{2,1,0:T(8,128)} %scatter_fusion.1, s32[8]{0:T(128)S(1)} %fusion.48, f32[8,128,768]{2,1,0:T(8,128)} %bitcast_select_fusion.1), kind=kCustom, calls=%fused_computation.7 | custom fusion | flops 786432 | bytes 9437216 | tf_op jit(solution)/shard_map/scatter-add | solution.py:45
  400.7 3.4 scatter_fusion.3
  404.1 28.1 %all-reduce.4.cloned.1.call-done = f32[768,768]{1,0:T(8,128)} async-done(((f32[768,768]{1,0:T(8,128)}), f32[768,768]{1,0:T(8,128)}) %all-reduce.4.cloned.1.call-update) | async-done | bytes 2359312 | tf_op jit(solution)/shard_map/psum | solution.py:181
  (118 shorter events, 53.8 us)
Async XLA Ops:
  7.2 135.0 %copy-start = (f32[768,768]{1,0:T(8,128)S(1)}, f32[768,768]{1,0:T(8,128)}, u32[]{:S(2)}) copy-start(f32[768,768]{1,0:T(8,128)} %param.10) | copy-start | bytes 7077892
  15.3 25.1 %all-to-all-start.1 = ((bf16[4,2,128,768]{3,2,1,0:T(8,128)(2,1)}), bf16[4,2,128,768]{3,2,1,0:T(8,128)(2,1)}, u32[]{:S(2)}, u32[]{:S(2)}) async-start(bf16[4,2,128,768]{3,2,1,0:T(8,128)(2,1)} %select_select_fusion.1), calls=%async_computation.1 | async-start | bytes 3145728 | tf_op jit(solution)/shard_map/all_to_all | solution.py:112
  27.9 19.4 %copy-start.8 = (s32[32]{0:T(128)S(1)}, s32[32]{0:T(128)}, u32[]{:S(2)}) copy-start(s32[32]{0:T(128)} %param.12) | copy-start | bytes 388
  27.9 21.5 %copy-start.10 = (u32[32]{0:T(128)S(1)}, u32[32]{0:T(128)}, u32[]{:S(2)}) copy-start(u32[32]{0:T(128)} %constant.215) | copy-start | bytes 388
  27.9 25.5 %copy-start.9 = (s32[32]{0:T(128)S(1)}, s32[32]{0:T(128)}, u32[]{:S(2)}) copy-start(s32[32]{0:T(128)} %param.13) | copy-start | bytes 388
  27.9 90.8 %copy-start.3 = (f32[32,768]{1,0:T(8,128)S(1)}, f32[32,768]{1,0:T(8,128)}, u32[]{:S(2)}) copy-start(f32[32,768]{1,0:T(8,128)} %param.11) | copy-start | bytes 294916
  40.4 86.4 %all-to-all-start = ((bf16[8,2,128,768]{3,2,1,0:T(8,128)(2,1)}), bf16[8,2,128,768]{3,2,1,0:T(8,128)(2,1)}, u32[]{:S(2)}, u32[]{:S(2)}) async-start(bf16[8,2,128,768]{3,2,1,0:T(8,128)(2,1)} %select_select_fusion), calls=%async_computation | async-start | bytes 6291456 | tf_op jit(solution)/shard_map/all_to_all | solution.py:104
  47.1 211.4 %reduce-scatter.5.cloned.1.call-start = ((), (), s32[]{:S(2)}) async-start(), calls=%async_computation.8 | async-start | bytes 491520 | tf_op jit(solution)/shard_map/reduce_scatter | solution.py:165
  142.2 35.8 %copy-start.6 = (f32[32,768]{1,0:T(8,128)}, f32[32,768]{1,0:T(8,128)S(1)}, u32[]{:S(2)}) copy-start(f32[32,768]{1,0:T(8,128)S(1)} %fusion.7) | copy-start | bytes 294916
  142.2 33.8 %copy-start.2 = (f32[128,768]{1,0:T(8,128)S(1)}, f32[128,768]{1,0:T(8,128)}, u32[]{:S(2)}) copy-start(f32[128,768]{1,0:T(8,128)} %all_gather.16) | copy-start | bytes 1179652
  205.6 52.9 %copy-start.4 = (f32[32,768]{1,0:T(8,128)S(1)}, f32[32,768]{1,0:T(8,128)}, u32[]{:S(2)}) copy-start(f32[32,768]{1,0:T(8,128)} %param.11) | copy-start | bytes 294916
  205.6 86.2 %copy-start.7 = (f32[32,768]{1,0:T(8,128)S(1)}, f32[32,768]{1,0:T(8,128)}, u32[]{:S(2)}) copy-start(f32[32,768]{1,0:T(8,128)} %copy-done.6) | copy-start | bytes 294916
  205.6 85.1 %reduce-scatter.3.cloned.1.call-start = ((), (), s32[]{:S(2)}) async-start(), calls=%async_computation.6 | async-start | bytes 884736 | tf_op jit(solution)/shard_map/reduce_scatter | solution.py:161
  209.4 153.1 %all-to-all-start.2 = ((bf16[8,2,32,128]{3,2,1,0:T(8,128)(2,1)}), bf16[8,2,32,128]{3,2,1,0:T(8,128)(2,1)S(1)}, u32[]{:S(2)}, u32[]{:S(2)}) async-start(bf16[8,2,32,128]{3,2,1,0:T(8,128)(2,1)} %copy.27), calls=%async_computation.3 | async-start | bytes 262144 | tf_op jit(solution)/shard_map/all_to_all | solution.py:189
  212.8 219.4 %all-reduce.4.cloned.1.call-start = ((), (), s32[]{:S(2)}) async-start(), calls=%async_computation.7 | async-start | bytes 4718592 | tf_op jit(solution)/shard_map/psum | solution.py:181
  290.7 5.6 %copy-start.5 = (f32[32,768]{1,0:T(8,128)S(1)}, f32[32,768]{1,0:T(8,128)}, u32[]{:S(2)}) copy-start(f32[32,768]{1,0:T(8,128)} %reduce-scatter.3.cloned.1.call-done) | copy-start | bytes 294916
  362.5 28.0 %all-to-all-start.3 = ((bf16[4,2,32,128]{3,2,1,0:T(8,128)(2,1)}), bf16[4,2,32,128]{3,2,1,0:T(8,128)(2,1)S(1)}, u32[]{:S(2)}, u32[]{:S(2)}) async-start(bf16[4,2,32,128]{3,2,1,0:T(8,128)(2,1)} %copy.30), calls=%async_computation.4 | async-start | bytes 131072 | tf_op jit(solution)/shard_map/all_to_all | solution.py:205
  400.7 34.8 %copy-start.1 = (f32[768,768]{1,0:T(8,128)S(1)}, f32[768,768]{1,0:T(8,128)}, u32[]{:S(2)}) copy-start(f32[768,768]{1,0:T(8,128)} %param.10) | copy-start | bytes 7077892
Sparse Core Ops, SparseCore 0:
  205.7 17.4 reduce-scatter.4
  227.1 63.5 reduce-scatter.2
  296.8 135.3 all-reduce.3
where the time goes:
time: 445 us; the launch traced here: 443 us
  blocking collectives  206 us (46%)
  other arithmetic  78.7 us (18%)
  waiting for transfers between devices  70.1 us (16%)
  matrix products  27 us (6%)
  local copies, waits for them, and re-layouts  25.3 us (6%)
  between operations  18.5 us (4%)
  starting transfers between devices  17.8 us (4%)
    unnamed x1, blocking collectives  64.1 us
    psum x1, blocking collectives, shards(): lax.psum((jnp.sum(jnp.log(own_rows)) + jnp.sum(jnp.log(own_cols)), positi...  40.7 us
    all_gather x1, blocking collectives, shards(): lax.all_gather(unit_nodes, 'dev', axis=0, tiled=True)  32.1 us
    all_gather x1, blocking collectives, shards(): lax.all_gather(rounded_grads, 'dev', axis=0, tiled=True)  31.2 us
    reduce_scatter x1, waiting for transfers between devices, shards(): lax.psum_scatter(node_part, 'dev', scatter_dimension=0, tiled=True)  29.5 us
    psum x1, waiting for transfers between devices, shards(): grad_weight = lax.psum(weight_term, ('grp', 'dev'))  28.1 us
    scatter-add x1, other arithmetic, shards(): grad_blocks = empty_blocks.at[col_block].add(local_spread)  25.5 us
    scatter-add x2, other arithmetic, land_blocks(): total.at[block_index].add(jnp.where(valid[:, None, None], incoming, 0.0))  22 us
  transfers between devices with their start and end apart: 7, of which 3 were waited for; matrix products, arithmetic and copies ran while one was open for 22% of the time, Pallas kernels for 0%

commit v1 on v0

--- a/solution.py
+++ b/solution.py
@@ -9,6 +9,11 @@
 PRECISE = lax.Precision.HIGHEST
 ROOT_HALF = 0.7071067811865476
 INV_ROOT_TWO_PI = 0.3989422804014327
+
+
+def summed_here(block, name):
+    blocks = lax.all_gather(block, name)
+    return jnp.sum(blocks, axis=0)
 
 
 def gelu_value(value):
@@ -178,7 +183,7 @@
     ) / text_norm
     pre_grad = node_back * gelu_slope(before)
     weight_term = lax.dot_general(chosen, pre_grad, (((0,), (0,)), ((), ())), precision=PRECISE)
-    grad_weight = lax.psum(weight_term, ("grp", "dev"))
+    grad_weight = summed_here(weight_term, ("grp", "dev"))
     row_grads = lax.dot_general(pre_grad, weight, (((1,), (1,)), ((), ())), precision=PRECISE)
     rounded_grads = row_grads.astype(jnp.bfloat16)
     empty_blocks = jnp.zeros((blocks_dev, block_rows, feat_width), jnp.float32)

time: 445 us -> 725 us (1.63)
  waiting for transfers between devices: 70.1 us -> 322 us
  other arithmetic: 78.7 us -> 104 us
    all_gather x0 -> x1, waiting for transfers between devices: none -> 252 us  [summed_here(): blocks = lax.all_gather(block, name)]
    psum x1 -> x0, waiting for transfers between devices: 28.1 us -> none  [shards(): grad_weight = lax.psum(weight_term, ('grp', 'dev'))]
    reduce_scatter x1, waiting for transfers between devices: 29.5 us -> 57.5 us  [shards(): lax.psum_scatter(node_part, 'dev', scatter_dimension=0, tiled=True)]
    reduce_sum x0 -> x1, other arithmetic: none -> 25.1 us  [summed_here(): return jnp.sum(blocks, axis=0)]
  transfers between devices with their start and end apart: 7 -> 7, of which waited for: 3 -> 3; matrix products, arithmetic and copies ran while one was open for 22% -> 14% of each run, Pallas kernels for 0% -> 0%
where the time goes in v1:
time: 725 us; the launch traced here: 723 us
  waiting for transfers between devices  322 us (44%)
  blocking collectives  212 us (29%)
  other arithmetic  104 us (14%)
  matrix products  27.1 us (4%)
  local copies, waits for them, and re-layouts  22.1 us (3%)
  starting transfers between devices  18.6 us (3%)
  between operations  18.5 us (3%)
    all_gather x1, waiting for transfers between devices, summed_here(): blocks = lax.all_gather(block, name)  252 us
    unnamed x1, blocking collectives  64 us
    reduce_scatter x1, waiting for transfers between devices, shards(): lax.psum_scatter(node_part, 'dev', scatter_dimension=0, tiled=True)  57.5 us
    psum x1, blocking collectives, shards(): lax.psum((jnp.sum(jnp.log(own_rows)) + jnp.sum(jnp.log(own_cols)), positi...  43.3 us
    all_gather x1, blocking collectives, shards(): lax.all_gather(rounded_grads, 'dev', axis=0, tiled=True)  33.3 us
    all_gather x1, blocking collectives, shards(): lax.all_gather(unit_nodes, 'dev', axis=0, tiled=True)  32.1 us
    scatter-add x1, other arithmetic, shards(): grad_blocks = empty_blocks.at[col_block].add(local_spread)  25.3 us
    reduce_sum x1, other arithmetic, summed_here(): return jnp.sum(blocks, axis=0)  25.1 us
  transfers between devices with their start and end apart: 7, of which 3 were waited for; matrix products, arithmetic and copies ran while one was open for 14% of the time, Pallas kernels for 0%

profile of v1, /device:TPU:0, one launch (start us, length us, event | category | flops | bytes accessed | tf_op | source)
XLA Modules:
  0.0 723.3 jit_solution(17102007510393398845)
XLA Ops:
  15.3 4.4 all-to-all-start.1
  23.9 4.0 select_select_fusion
  27.9 12.5 %all-to-all-done.1 = bf16[4,2,128,768]{3,2,1,0:T(8,128)(2,1)} async-done(((bf16[4,2,128,768]{3,2,1,0:T(8,128)(2,1)}), bf16[4,2,128,768]{3,2,1,0:T(8,128)(2,1)}, u32[]{:S(2)}, u32[]{:S(2)}) %all-to-all-start.1) | async-done | bytes 1572896 | tf_op jit(solution)/shard_map/all_to_all | solution.py:117
  40.4 6.6 all-to-all-start
  53.7 64.0 %all-reduce = s32[256]{0:T(256)S(1)} all-reduce(s32[256]{0:T(256)S(1)} %dynamic-update-slice), channel_id=1, replica_groups=mesh['grp'=4,'dev'=8] {'dev'}, use_global_device_ids=true, to_apply=%add | all-reduce | flops 256 | bytes 2048
  119.0 6.6 all_gather.22
  126.8 5.8 pad_maximum_fusion
  132.6 6.0 gather_fusion.4
  143.9 32.1 %all_gather.21 = f32[256,768]{1,0:T(8,128)S(1)} all-gather(f32[32,768]{1,0:T(8,128)S(1)} %broadcast_divide_fusion.1), channel_id=1, replica_groups=mesh['grp'=4,'dev'=8] {'dev'}, dimensions={0}, use_global_device_ids=true | all-gather | bytes 884736 | tf_op jit(solution)/shard_map/all_gather | solution.py:147
  178.0 19.6 %psum.28 = f32[256]{0:T(256)S(1)} all-reduce(f32[256]{0:T(256)S(1)} %get-tuple-element.6), channel_id=1, replica_groups=mesh['grp'=4,'dev'=8] {'dev'}, use_global_device_ids=true, to_apply=%region_10.11 | all-reduce | flops 256 | bytes 2048 | tf_op jit(solution)/shard_map/psum | solution.py:155
  197.6 5.6 psum.29
  208.6 57.5 %reduce-scatter.3.cloned.1.call-done = f32[32,768]{1,0:T(8,128)} async-done(((f32[256,768]{1,0:T(8,128)}), f32[32,768]{1,0:T(8,128)}) %reduce-scatter.3.cloned.1.call-update) | async-done | bytes 98320 | tf_op jit(solution)/shard_map/reduce_scatter | solution.py:166
  267.2 4.5 fusion.57
  272.6 3.7 all-to-all-start.2
  279.9 43.3 %all-reduce.1 = (f32[]{:T(128)}, f32[]{:T(128)}) all-reduce(f32[]{:T(128)S(6)} %add.308, f32[]{:T(128)} %get-tuple-element.4), channel_id=1, replica_groups=mesh['grp'=4,'dev'=8] {'grp','dev'}, use_global_device_ids=true, to_apply=%region_15.16 | all-reduce | flops 2 | bytes 16 | tf_op jit(solution)/shard_map/psum | solution.py:174
  329.6 6.1 fusion.12
  336.9 25.3 %scatter_fusion = f32[4,128,768]{2,1,0:T(8,128)} fusion(f32[4,128,768]{2,1,0:T(8,128)} %broadcast_in_dim.214, s32[28]{0:T(128)S(1)} %get-tuple-element.15, f32[28,128,768]{2,1,0:T(8,128)} %fusion.12), kind=kCustom, calls=%fused_computation.5 | custom fusion | flops 2752512 | bytes 33030256 | tf_op jit(solution)/shard_map/scatter-add | solution.py:193
  362.3 33.3 %all_gather.24 = bf16[256,768]{1,0:T(8,128)(2,1)S(1)} all-gather(bf16[32,768]{1,0:T(8,128)(2,1)S(1)} %get-tuple-element.34), channel_id=1, replica_groups=mesh['grp'=4,'dev'=8] {'dev'}, dimensions={0}, use_global_device_ids=true | all-gather | bytes 442368 | tf_op jit(solution)/shard_map/all_gather | solution.py:201
  395.6 3.7 all-to-all-start.3
  403.8 14.6 %scatter_fusion.1 = f32[4,128,768]{2,1,0:T(8,128)} fusion(f32[4,128,768]{2,1,0:T(8,128)} %scatter_fusion, s32[16]{0:T(128)S(1)} %fusion.47, f32[16,128,768]{2,1,0:T(8,128)} %bitcast_select_fusion), kind=kCustom, calls=%fused_computation.6 | custom fusion | flops 1572864 | bytes 18874432 | tf_op jit(solution)/shard_map/scatter-add | solution.py:50
  418.4 7.1 all_gather.25
  428.2 7.4 %scatter_fusion.2 = f32[4,128,768]{2,1,0:T(8,128)} fusion(f32[4,128,768]{2,1,0:T(8,128)} %scatter_fusion.1, s32[8]{0:T(128)S(1)} %fusion.48, f32[8,128,768]{2,1,0:T(8,128)} %bitcast_select_fusion.1), kind=kCustom, calls=%fused_computation.7 | custom fusion | flops 786432 | bytes 9437216 | tf_op jit(solution)/shard_map/scatter-add | solution.py:50
  439.1 251.5 %all-gather.3.cloned.1.call-done = f32[24576,768]{1,0:T(8,128)} async-done(((f32[768,768]{1,0:T(8,128)}), f32[24576,768]{1,0:T(8,128)}) %all-gather.3.cloned.1.call-update) | async-done | bytes 75497488 | tf_op jit(solution)/shard_map/all_gather | solution.py:15
  690.6 25.1 %reduce_sum.131 = f32[768,768]{1,0:T(8,128)} reduce(f32[32,768,768]{2,1,0:T(8,128)} %bitcast.36, f32[]{:T(128)} %constant.203.clone.1), dimensions={0}, to_apply=%region_24.25 | reduce | flops 18284544 | bytes 77856768 | tf_op jit(solution)/shard_map/reduce_sum | solution.py:16
  (116 shorter events, 54.4 us)
Async XLA Ops:
  7.2 135.0 %copy-start = (f32[768,768]{1,0:T(8,128)S(1)}, f32[768,768]{1,0:T(8,128)}, u32[]{:S(2)}) copy-start(f32[768,768]{1,0:T(8,128)} %param.10) | copy-start | bytes 7077892
  15.3 25.1 %all-to-all-start.1 = ((bf16[4,2,128,768]{3,2,1,0:T(8,128)(2,1)}), bf16[4,2,128,768]{3,2,1,0:T(8,128)(2,1)}, u32[]{:S(2)}, u32[]{:S(2)}) async-start(bf16[4,2,128,768]{3,2,1,0:T(8,128)(2,1)} %select_select_fusion.1), calls=%async_computation.1 | async-start | bytes 3145728 | tf_op jit(solution)/shard_map/all_to_all | solution.py:117
  27.9 19.2 %copy-start.7 = (s32[32]{0:T(128)S(1)}, s32[32]{0:T(128)}, u32[]{:S(2)}) copy-start(s32[32]{0:T(128)} %param.12) | copy-start | bytes 388
  27.9 24.3 %copy-start.9 = (u32[32]{0:T(128)S(1)}, u32[32]{0:T(128)}, u32[]{:S(2)}) copy-start(u32[32]{0:T(128)} %constant.215) | copy-start | bytes 388
  27.9 25.5 %copy-start.8 = (s32[32]{0:T(128)S(1)}, s32[32]{0:T(128)}, u32[]{:S(2)}) copy-start(s32[32]{0:T(128)} %param.13) | copy-start | bytes 388
  27.9 90.8 %copy-start.3 = (f32[32,768]{1,0:T(8,128)S(1)}, f32[32,768]{1,0:T(8,128)}, u32[]{:S(2)}) copy-start(f32[32,768]{1,0:T(8,128)} %param.11) | copy-start | bytes 294916
  40.4 86.4 %all-to-all-start = ((bf16[8,2,128,768]{3,2,1,0:T(8,128)(2,1)}), bf16[8,2,128,768]{3,2,1,0:T(8,128)(2,1)}, u32[]{:S(2)}, u32[]{:S(2)}) async-start(bf16[8,2,128,768]{3,2,1,0:T(8,128)(2,1)} %select_select_fusion), calls=%async_computation | async-start | bytes 6291456 | tf_op jit(solution)/shard_map/all_to_all | solution.py:109
  47.1 219.0 %reduce-scatter.3.cloned.1.call-start = ((), (), s32[]{:S(2)}) async-start(), calls=%async_computation.6 | async-start | bytes 884736 | tf_op jit(solution)/shard_map/reduce_scatter | solution.py:166
  142.2 35.8 %copy-start.6 = (f32[32,768]{1,0:T(8,128)}, f32[32,768]{1,0:T(8,128)S(1)}, u32[]{:S(2)}) copy-start(f32[32,768]{1,0:T(8,128)S(1)} %fusion.7) | copy-start | bytes 294916
  142.2 33.8 %copy-start.2 = (f32[128,768]{1,0:T(8,128)S(1)}, f32[128,768]{1,0:T(8,128)}, u32[]{:S(2)}) copy-start(f32[128,768]{1,0:T(8,128)} %all_gather.22) | copy-start | bytes 1179652
  206.1 118.5 %reduce-scatter.5.cloned.1.call-start = ((), (), s32[]{:S(2)}) async-start(), calls=%async_computation.7 | async-start | bytes 491520 | tf_op jit(solution)/shard_map/reduce_scatter | solution.py:170
  208.5 482.1 %all-gather.3.cloned.1.call-start = ((), (), s32[]{:S(2)}) async-start(), calls=%async_computation.8 | async-start | bytes 77856768 | tf_op jit(solution)/shard_map/all_gather | solution.py:15
  267.2 57.4 %copy-start.4 = (f32[32,768]{1,0:T(8,128)S(1)}, f32[32,768]{1,0:T(8,128)}, u32[]{:S(2)}) copy-start(f32[32,768]{1,0:T(8,128)} %param.11) | copy-start | bytes 294916
  267.2 60.1 %copy-start.5 = (f32[32,768]{1,0:T(8,128)S(1)}, f32[32,768]{1,0:T(8,128)}, u32[]{:S(2)}) copy-start(f32[32,768]{1,0:T(8,128)} %reduce-scatter.3.cloned.1.call-done) | copy-start | bytes 294916
  272.6 123.0 %all-to-all-start.2 = ((bf16[8,2,32,128]{3,2,1,0:T(8,128)(2,1)}), bf16[8,2,32,128]{3,2,1,0:T(8,128)(2,1)S(1)}, u32[]{:S(2)}, u32[]{:S(2)}) async-start(bf16[8,2,32,128]{3,2,1,0:T(8,128)(2,1)} %copy.27), calls=%async_computation.3 | async-start | bytes 262144 | tf_op jit(solution)/shard_map/all_to_all | solution.py:194
  395.6 30.0 %all-to-all-start.3 = ((bf16[4,2,32,128]{3,2,1,0:T(8,128)(2,1)}), bf16[4,2,32,128]{3,2,1,0:T(8,128)(2,1)S(1)}, u32[]{:S(2)}, u32[]{:S(2)}) async-start(bf16[4,2,32,128]{3,2,1,0:T(8,128)(2,1)} %copy.30), calls=%async_computation.4 | async-start | bytes 131072 | tf_op jit(solution)/shard_map/all_to_all | solution.py:210
  690.6 25.1 %copy-start.1 = (f32[768,768]{1,0:T(8,128)S(1)}, f32[768,768]{1,0:T(8,128)}, u32[]{:S(2)}) copy-start(f32[768,768]{1,0:T(8,128)} %param.10) | copy-start | bytes 7077892
Sparse Core Ops, SparseCore 0:
  206.2 59.8 reduce-scatter.2
  268.6 20.0 reduce-scatter.4
  292.2 398.3 all-gather.2
